TPU v7x, 512 devices: a whole 4x8x8 slice. The times are simulated.
512 devices in a mesh: share: 16 (over z, core), row: 32 (over y, x).
Axes of the slice: x: 4, y: 8, z: 8, core: 2. Of those that a mesh axis runs over, the one named last changes fastest.
Arguments:
- remaining_coded_pieces: float32 [16, 512, 8192], P('share', 'row'), may hold values from -6 to 6
- alive_piece_indices: int32 [16], replicated, may hold values from 0 to 19, as said below
- slab_starting_positions: int32 [2], replicated, may hold values from 0 to 48
Outputs:
- decoded: float32 [16, 512, 4096], P('share', None, 'row')
Inputs may be any that keep to these rules, and one draw needn't show every extreme that they name: `alive_piece_indices`: 16 different share numbers in rising order.
All inputs are finite; a program needn't handle non-finite values.
Results may differ from a plain program's by a relative error of at most 0.00007.
Values sent between devices are 32-bit elements; how exact they have to be, the bound alone decides.
A program may use at most 64 MiB of HBM per device.

v0:
```python
import jax
import jax.numpy as jnp
from jax import lax
from jax.sharding import Mesh
from jax.sharding import PartitionSpec as P

K = 16
CODED_PIECES_ALL = 20
W = 2048
ROW = ("row_0", "row_1")


def in_blocks(shard, dim, count):
    before, after = (shard.shape[:dim], shard.shape[dim + 1 :])
    return jnp.moveaxis(shard.reshape(*before, count, -1, *after), dim, 0)


def in_order(pieces, dim):
    pieces = jnp.moveaxis(pieces, 0, dim)
    shape = pieces.shape
    return pieces.reshape(*shape[:dim], shape[dim] * shape[dim + 1], *shape[dim + 2 :])


def exchange_in_order(pieces, axes, order):
    inside = pieces.shape[1:]
    filled = pieces.reshape(*(lax.axis_size(a) for a in axes), *inside)
    for k in order:
        filled = lax.all_to_all(filled, axes[k], k, k, tiled=True)
    return filled.reshape(-1, *inside)


def exchange_by_axis(shard, axes, order, split_dim, concat_dim):
    pieces = in_blocks(shard, split_dim, lax.axis_size(axes))
    return in_order(exchange_in_order(pieces, axes, order), concat_dim)


def recovery_operator(alive_piece_indices):
    numbers = jnp.arange(CODED_PIECES_ALL, dtype=jnp.float32)
    nodes = jnp.cos(jnp.pi * (2.0 * numbers + 1.0) / (2.0 * CODED_PIECES_ALL))
    chosen_coded_pieces = (
        alive_piece_indices[:, None] == jnp.arange(CODED_PIECES_ALL, dtype=jnp.int32)[None, :]
    ).astype(jnp.float32)
    points = jnp.sum(chosen_coded_pieces * nodes[None, :], axis=1)
    polynomial_degrees = jnp.arange(K, dtype=jnp.float32)
    angles = jnp.pi * (2.0 * polynomial_degrees + 1.0) / (2.0 * K)
    samples = jnp.cos(angles)
    same = jnp.arange(K, dtype=jnp.int32)[:, None] == jnp.arange(K, dtype=jnp.int32)[None, :]
    spacing = jnp.where(same, 1.0, points[:, None] - points[None, :])
    factors = (samples[None, None, :] - points[None, :, None]) / spacing[:, :, None]
    factors = jnp.where(same[:, :, None], 1.0, factors)
    lagrange = jnp.prod(factors, axis=1)
    table = jnp.cos(polynomial_degrees[:, None] * angles[None, :])
    recovery_coefficients = 2.0 / K * jnp.sum(table[:, None, :] * lagrange[None, :, :], axis=2)
    return recovery_coefficients * jnp.where(polynomial_degrees == 0.0, 0.5, 1.0)[:, None]


def body(remaining_coded_pieces, alive_piece_indices, slab_starting_positions):
    recovery_coefficients = recovery_operator(alive_piece_indices)
    first = lax.dynamic_slice_in_dim(remaining_coded_pieces, slab_starting_positions[0] * 128, W, 2)
    second = lax.dynamic_slice_in_dim(
        remaining_coded_pieces, slab_starting_positions[1] * 128, W, 2
    )
    slabs = jnp.concatenate([first, second], axis=2)
    spread = exchange_by_axis(slabs, ROW, (0, 1), 2, 1)
    mixed = jnp.einsum(
        "ki,irc->krc",
        recovery_coefficients,
        lax.all_to_all(spread, "share", split_axis=1, concat_axis=0, tiled=True),
        precision=lax.Precision.HIGHEST,
    )
    decoded = lax.all_to_all(mixed, "share", split_axis=0, concat_axis=1, tiled=True)
    return decoded


def solution(mesh):
    torus = Mesh(mesh.devices.reshape(mesh.shape["share"], 8, 4), ("share", "row_0", "row_1"))
    in_specs = (P("share", ROW, None), P(), P())
    out_specs = P("share", None, ROW)
    return jax.shard_map(body, mesh=torus, in_specs=in_specs, out_specs=out_specs, check_vma=False)
```

profile of v0, /device:TPU:1, one launch (start us, length us, event | category | flops | bytes accessed | tf_op | source)
XLA Modules:
  0.0 74.8 jit_solution(10158319778177001810)
XLA Ops:
  0.0 1.3 %fusion.8 = (s32[1]{0:T(128)}, s32[1]{0:T(128)}) fusion(s32[2]{0:T(128)} %param.5), kind=kLoop, calls=%fused_computation.23 | loop fusion | bytes 16 | tf_op jit(solution)/shard_map/slice | solution.py:59
  2.6 1.0 %constant_dynamic-slice_fusion.1 = (f32[1,16,2048]{2,1,0:T(8,128)S(1)}, f32[1,16,2048]{2,1,0:T(8,128)S(1)}) fusion(f32[1,16,8192]{2,1,0:T(8,128)} %param.3, s32[]{:T(128)S(6)} %select_n.29, s32[]{:T(128)S(6)} %select_n.30), kind=kLoop, calls=%fused_computation.19 | loop fusion | bytes 524296 | tf_op jit(solution)/shard_map/dynamic_slice | solution.py:59
  3.6 0.7 copy_bitcast_fusion
  4.4 7.6 %all-to-all-start = ((f32[8,4,1,16,128]{4,3,1,2,0:T(8,128)}), f32[8,4,1,16,128]{4,3,1,2,0:T(8,128)S(1)}, u32[]{:S(2)}, u32[]{:S(2)}) async-start(f32[8,4,1,16,128]{4,3,1,2,0:T(8,128)} %bitcast.4), calls=%async_computation | async-start | bytes 524288 | tf_op jit(solution)/shard_map/all_to_all | solution.py:28
  12.1 0.0 copy-start
  12.1 0.6 copy-done
  12.8 0.2 select_reduce_fusion
  13.0 8.5 %all-to-all-done = f32[8,4,1,16,128]{4,3,1,2,0:T(8,128)S(1)} async-done(((f32[8,4,1,16,128]{4,3,1,2,0:T(8,128)}), f32[8,4,1,16,128]{4,3,1,2,0:T(8,128)S(1)}, u32[]{:S(2)}, u32[]{:S(2)}) %all-to-all-start) | async-done | bytes 262176 | tf_op jit(solution)/shard_map/all_to_all | solution.py:28
  21.4 0.7 copy.14
  22.2 5.1 %all-to-all-start.1 = ((f32[8,4,1,16,128]{4,3,0,2,1:T(8,128)}), f32[8,4,1,16,128]{4,3,0,2,1:T(8,128)S(1)}, u32[]{:S(2)}, u32[]{:S(2)}) async-start(f32[8,4,1,16,128]{4,3,0,2,1:T(8,128)} %copy.14), calls=%async_computation.1 | async-start | bytes 524288 | tf_op jit(solution)/shard_map/all_to_all | solution.py:28
  27.2 0.1 broadcast_subtract_fusion
  27.3 5.5 %all-to-all-done.1 = f32[8,4,1,16,128]{4,3,0,2,1:T(8,128)S(1)} async-done(((f32[8,4,1,16,128]{4,3,0,2,1:T(8,128)}), f32[8,4,1,16,128]{4,3,0,2,1:T(8,128)S(1)}, u32[]{:S(2)}, u32[]{:S(2)}) %all-to-all-start.1) | async-done | bytes 262176 | tf_op jit(solution)/shard_map/all_to_all | solution.py:28
  32.8 0.7 copy.15
  33.5 14.1 %all-to-all-start.2 = ((f32[1,512,128]{2,0,1:T(1,128)}), f32[1,512,128]{2,0,1:T(1,128)S(1)}, u32[]{:S(2)}, u32[]{:S(2)}) async-start(f32[1,512,128]{2,0,1:T(1,128)} %bitcast.6), calls=%async_computation.2 | async-start | bytes 524288 | tf_op jit(solution)/shard_map/all_to_all | solution.py:68
  47.6 0.1 fusion.2
  47.7 0.1 multiply_cosine_fusion
  47.8 0.1 multiply_reduce_fusion
  47.9 11.3 %all-to-all-done.2 = f32[1,512,128]{2,0,1:T(1,128)S(1)} async-done(((f32[1,512,128]{2,0,1:T(1,128)}), f32[1,512,128]{2,0,1:T(1,128)S(1)}, u32[]{:S(2)}, u32[]{:S(2)}) %all-to-all-start.2) | async-done | bytes 262176 | tf_op jit(solution)/shard_map/all_to_all | solution.py:68
  59.2 0.5 fusion
  59.7 0.1 copy.18
  59.8 14.4 %all_to_all.34 = f32[16,32,128]{2,1,0:T(8,128)S(1)} all-to-all(f32[16,32,128]{2,1,0:T(8,128)S(1)} %copy.18), channel_id=1, replica_groups=mesh['share'=16,'row_0'=8,'row_1'=4] {'share'}, dimensions={0} | all-to-all | bytes 524288 | tf_op jit(solution)/shard_map/all_to_all | solution.py:71
  74.1 0.7 copy.24
  (5 shorter events, 0.1 us)
Async XLA Ops:
  4.4 17.1 %all-to-all-start = ((f32[8,4,1,16,128]{4,3,1,2,0:T(8,128)}), f32[8,4,1,16,128]{4,3,1,2,0:T(8,128)S(1)}, u32[]{:S(2)}, u32[]{:S(2)}) async-start(f32[8,4,1,16,128]{4,3,1,2,0:T(8,128)} %bitcast.4), calls=%async_computation | async-start | bytes 524288 | tf_op jit(solution)/shard_map/all_to_all | solution.py:28
  12.1 0.7 copy-start
  22.2 10.6 %all-to-all-start.1 = ((f32[8,4,1,16,128]{4,3,0,2,1:T(8,128)}), f32[8,4,1,16,128]{4,3,0,2,1:T(8,128)S(1)}, u32[]{:S(2)}, u32[]{:S(2)}) async-start(f32[8,4,1,16,128]{4,3,0,2,1:T(8,128)} %copy.14), calls=%async_computation.1 | async-start | bytes 524288 | tf_op jit(solution)/shard_map/all_to_all | solution.py:28
  33.5 25.7 %all-to-all-start.2 = ((f32[1,512,128]{2,0,1:T(1,128)}), f32[1,512,128]{2,0,1:T(1,128)S(1)}, u32[]{:S(2)}, u32[]{:S(2)}) async-start(f32[1,512,128]{2,0,1:T(1,128)} %bitcast.6), calls=%async_computation.2 | async-start | bytes 524288 | tf_op jit(solution)/shard_map/all_to_all | solution.py:68
where the time goes:
time: 75.3 us; the launch traced here: 74.8 us
  starting transfers between devices  26.8 us (36%)
  waiting for transfers between devices  25.2 us (33%)
  blocking collectives  14.4 us (19%)
  local copies, waits for them, and re-layouts  5.22 us (7%)
  other arithmetic  1.4 us (2%)
  between operations  1.36 us (2%)
    all_to_all x1, blocking collectives, body(): lax.all_to_all(mixed, 'share', split_axis=0, concat_axis=1, tiled=True)  14.4 us
    all_to_all x1, starting transfers between devices, body(): lax.all_to_all(spread, 'share', split_axis=1, concat_axis=0, tiled=True)  14.1 us
    all_to_all x2, waiting for transfers between devices, exchange_in_order(): filled = lax.all_to_all(filled, axes[k], k, k, tiled=True)  13.9 us
    all_to_all x2, starting transfers between devices, exchange_in_order(): filled = lax.all_to_all(filled, axes[k], k, k, tiled=True)  12.7 us
    all_to_all x1, waiting for transfers between devices, body(): lax.all_to_all(spread, 'share', split_axis=1, concat_axis=0, tiled=True)  11.3 us
  transfers between devices with their start and end apart: 3, of which 3 were waited for; matrix products, arithmetic and copies ran while one was open for 1% of the time, Pallas kernels for 0%

commit v1 on v0

v1 whole, which is shorter than its diff:
```python
import functools

import jax
import jax.numpy as jnp
import numpy as np
from jax import lax
from jax.experimental import pallas as pl
from jax.experimental.pallas import tpu as pltpu
from jax.sharding import PartitionSpec as P

K = 16
CODED_PIECES_ALL = 20
W = 2048
LANES = 128
SUBLANES = 8
CHUNKS = 1
MESH = pl.DeviceIdType.MESH


def constants():
    table = np.zeros((24, LANES), np.float32)
    theta = np.pi * (2.0 * np.arange(K) + 1.0) / (2.0 * K)
    degrees = np.arange(K)[:, None]
    scale = np.where(degrees == 0, 1.0, 2.0) / K
    table[:K, :K] = scale * np.cos(degrees * theta[None, :])
    table[K, :K] = np.cos(theta)
    numbers = np.arange(CODED_PIECES_ALL)
    table[K + 1, :CODED_PIECES_ALL] = np.cos(np.pi * (2.0 * numbers + 1.0) / (2.0 * CODED_PIECES_ALL))
    return table


def weights_into(table, alive, points_ref, w_ref):
    rows = lax.broadcasted_iota(jnp.int32, (K, LANES), 0)
    lanes = lax.broadcasted_iota(jnp.int32, (K, LANES), 1)
    number = jnp.zeros((K, LANES), jnp.int32)
    for i in range(K):
        number = jnp.where(rows == i, alive[i], number)
    nodes = jnp.broadcast_to(table[K + 1 : K + 2, :], (K, LANES))
    points = jnp.sum(jnp.where(lanes == number, nodes, 0.0), axis=1, keepdims=True)
    points = jnp.broadcast_to(points, (K, LANES))
    points_ref[...] = points
    samples = table[K : K + 1, :]
    over = jnp.ones((K, LANES), jnp.float32)
    under = jnp.ones((K, LANES), jnp.float32)
    for j in range(K):
        point = points_ref[j : j + 1, :]
        over = over * jnp.where(rows == j, 1.0, samples - point)
        under = under * jnp.where(rows == j, 1.0, points - point)
    lagrange = over / under
    for k in range(K):
        total = jnp.sum(lagrange * table[k : k + 1, :], axis=1, keepdims=True)
        w_ref[k] = jnp.broadcast_to(total, (K, LANES))


def kernel(
    shares, rows, chunks,
    alive, starts, x_hbm, table_hbm, out,
    x, table, points, w, send_a, got_a, got_b, send_c,
    load_sems, a_send, a_recv, b_send, b_recv, c_send, c_recv,
):
    me_s = lax.axis_index("share")
    me_r = lax.axis_index("row")
    load_x = pltpu.make_async_copy(x_hbm, x, load_sems.at[0])
    load_t = pltpu.make_async_copy(table_hbm, table, load_sems.at[1])
    load_x.start()
    load_t.start()

    barrier = pltpu.get_barrier_semaphore()
    for d in range(1, rows):
        pl.semaphore_signal(barrier, inc=1, device_id=(me_s, lax.rem(me_r + d, rows)), device_id_type=MESH)
    for d in range(1, shares):
        pl.semaphore_signal(barrier, inc=1, device_id=(lax.rem(me_s + d, shares), me_r), device_id_type=MESH)

    tiles = x.shape[0] // chunks
    step = tiles * SUBLANES
    load_x.wait()
    for h in range(2):
        first = starts[h]
        for c in range(chunks):
            for t in range(tiles):
                for b in range(W // LANES):
                    block = x[c * tiles + t, first + b]
                    send_a[c, h * (W // LANES) + b, t * SUBLANES : (t + 1) * SUBLANES] = block
    pl.semaphore_wait(barrier, rows - 1 + shares - 1)

    for c in range(chunks):
        for d in range(1, rows):
            to = lax.rem(me_r + d, rows)
            pltpu.make_async_remote_copy(
                src_ref=send_a.at[c, to], dst_ref=got_a.at[c, me_r],
                send_sem=a_send, recv_sem=a_recv.at[c], device_id=(me_s, to), device_id_type=MESH,
            ).start()
    for c in range(chunks):
        got_a[c, me_r] = send_a[c, me_r]

    load_t.wait()
    weights_into(table, alive, points, w)

    def waits(ref, send, recv):
        return pltpu.make_async_remote_copy(
            src_ref=ref, dst_ref=ref, send_sem=send, recv_sem=recv, device_id=(me_s, me_r), device_id_type=MESH
        )

    for c in range(chunks):
        waits(got_a.at[c, pl.ds(0, rows - 1)], a_send, a_recv.at[c]).wait_recv()
        for d in range(1, shares):
            to = lax.rem(me_s + d, shares)
            pltpu.make_async_remote_copy(
                src_ref=got_a.at[c, pl.ds(2 * to, 2)], dst_ref=got_b.at[c, me_s],
                send_sem=b_send, recv_sem=b_recv.at[c], device_id=(to, me_r), device_id_type=MESH,
            ).start()
        got_b[c, me_s] = got_a[c, pl.ds(2 * me_s, 2)]

    for c in range(chunks):
        waits(got_b.at[c, pl.ds(0, shares - 1)], b_send, b_recv.at[c]).wait_recv()
        for h in range(2):
            data = [got_b[c, i, h] for i in range(K)]
            for k in range(K):
                total = w[k, 0:1, :] * data[0]
                for i in range(1, K):
                    total = total + w[k, i : i + 1, :] * data[i]
                send_c[c, k, h] = total
        for d in range(1, shares):
            to = lax.rem(me_s + d, shares)
            pltpu.make_async_remote_copy(
                src_ref=send_c.at[c, to], dst_ref=out.at[me_s, :, pl.ds(c * step, step)],
                send_sem=c_send, recv_sem=c_recv, device_id=(to, me_r), device_id_type=MESH,
            ).start()
        out[me_s, :, pl.ds(c * step, step)] = send_c[c, me_s]

    waits(got_a.at[:, pl.ds(0, rows - 1)], a_send, a_send).wait_send()
    waits(got_b.at[:, pl.ds(0, shares - 1)], b_send, b_send).wait_send()
    waits(send_c.at[:, pl.ds(0, shares - 1)], c_send, c_send).wait_send()
    waits(out.at[pl.ds(0, shares - 1)], c_send, c_recv).wait_recv()


def solution(mesh):
    shares, rows = mesh.shape["share"], mesh.shape["row"]
    table = constants()

    def body(remaining_coded_pieces, alive_piece_indices, slab_starting_positions):
        block, columns = remaining_coded_pieces.shape[1:]
        step = block // CHUNKS
        f32 = jnp.float32
        tiled = remaining_coded_pieces.reshape(block // SUBLANES, SUBLANES, columns // LANES, LANES).transpose(0, 2, 1, 3)
        dma = pltpu.SemaphoreType.DMA
        decoded = pl.pallas_call(
            functools.partial(kernel, shares, rows, CHUNKS),
            out_shape=jax.ShapeDtypeStruct((shares, 2, block, LANES), f32),
            in_specs=[
                pl.BlockSpec(memory_space=pltpu.SMEM),
                pl.BlockSpec(memory_space=pltpu.SMEM),
                pl.BlockSpec(memory_space=pl.ANY),
                pl.BlockSpec(memory_space=pl.ANY),
            ],
            out_specs=pl.BlockSpec(memory_space=pltpu.VMEM),
            scratch_shapes=[
                pltpu.VMEM((block // SUBLANES, columns // LANES, SUBLANES, LANES), f32),
                pltpu.VMEM((24, LANES), f32),
                pltpu.VMEM((K, LANES), f32),
                pltpu.VMEM((K, K, LANES), f32),
                pltpu.VMEM((CHUNKS, rows, step, LANES), f32),
                pltpu.VMEM((CHUNKS, rows, step, LANES), f32),
                pltpu.VMEM((CHUNKS, shares, 2, step, LANES), f32),
                pltpu.VMEM((CHUNKS, shares, 2, step, LANES), f32),
                dma((2,)),
                dma,
                dma((CHUNKS,)),
                dma,
                dma((CHUNKS,)),
                dma,
                dma,
            ],
            compiler_params=pltpu.CompilerParams(collective_id=0, has_side_effects=True),
            name="decode",
        )(alive_piece_indices, slab_starting_positions, tiled, jnp.asarray(table))
        return decoded.reshape(1, shares * 2 * block, LANES)

    return jax.shard_map(
        body, mesh=mesh, in_specs=(P("share", "row", None), P(), P()), out_specs=P("share", None, "row"), check_vma=False
    )
```

time: 75.3 us -> 45 us (0.60)
  Pallas kernels: 0 us -> 43.1 us
  starting transfers between devices: 26.8 us -> 0 us
  waiting for transfers between devices: 25.2 us -> 0 us
  blocking collectives: 14.4 us -> 0 us
  local copies, waits for them, and re-layouts: 5.22 us -> 1.67 us
  other arithmetic: 1.4 us -> 0 us
  between operations: 1.36 us -> 0.01 us
    pallas_call x0 -> x1, Pallas kernels: none -> 43.1 us  [body(): pl.pallas_call(functools.partial(kernel, shares, rows, CHUNKS), out_shape...]
    all_to_all x3 -> x0, starting transfers between devices: 26.8 us -> none  [the longest x1 14.1 us: body(): lax.all_to_all(spread, 'share', split_axis=1, concat_axis=0, tiled=True)]
    all_to_all x3 -> x0, waiting for transfers between devices: 25.2 us -> none  [the longest x2 13.9 us: exchange_in_order(): filled = lax.all_to_all(filled, axes[k], k, k, tiled=True)]
    all_to_all x1 -> x0, blocking collectives: 14.4 us -> none  [body(): lax.all_to_all(mixed, 'share', split_axis=0, concat_axis=1, tiled=True)]
    all_to_all x2 -> x0, local copies, waits for them, and re-layouts: 1.45 us -> none  [exchange_in_order(): filled = lax.all_to_all(filled, axes[k], k, k, tiled=True)]
    slice x1 -> x0, local copies, waits for them, and re-layouts: 1.34 us -> none  [body(): slab_starting_positions[0] * 128]
    dynamic_slice x1 -> x0, local copies, waits for them, and re-layouts: 1 us -> none  [body(): lax.dynamic_slice_in_dim(remaining_coded_pieces, slab_starting_positions[...]
    unnamed x3 -> x1, local copies, waits for them, and re-layouts: 1.34 us -> 1.67 us
  transfers between devices with their start and end apart: 3 -> 0, of which waited for: 3 -> 0; matrix products, arithmetic and copies ran while one was open for 1% -> 0% of each run, Pallas kernels for 0% -> 0%
where the time goes in v1:
time: 45 us; the launch traced here: 44.8 us
  Pallas kernels  43.1 us (96%)
  local copies, waits for them, and re-layouts  1.67 us (4%)
    pallas_call x1, Pallas kernels, body(): pl.pallas_call(functools.partial(kernel, shares, rows, CHUNKS), out_shape...  43.1 us
    unnamed x1, local copies, waits for them, and re-layouts  1.67 us

profile of v1, /device:TPU:1, one launch (start us, length us, event | category | flops | bytes accessed | tf_op | source)
XLA Modules:
  0.0 44.8 jit_solution(2371413115271012023)
XLA Ops:
  0.0 43.1 %decode.1 = f32[16,2,16,128]{3,2,1,0:T(8,128)} custom-call(s32[16]{0:T(128)} %alive.1, s32[2]{0:T(128)} %starts.1, f32[2,64,8,128]{3,2,1,0:T(8,128)} %bitcast.5, f32[24,128]{1,0:T(8,128)} %constant.2.clone.table_hbm), custom_call_target="tpu_custom_call" | custom-call | tf_op jit(solution)/shard_map/decode/pallas_call | solution.py:147
  43.2 1.7 %copy.6 = f32[1,512,128]{2,1,0:T(8,128)} copy(f32[1,512,128]{2,1,0:T(8,128)} %bitcast.4) | data formatting | bytes 524288

commit v2 on v1

v2 whole, which is shorter than its diff:
```python
import functools

import jax
import jax.numpy as jnp
import numpy as np
from jax import lax
from jax.experimental import pallas as pl
from jax.experimental.pallas import tpu as pltpu
from jax.sharding import PartitionSpec as P

K = 16
CODED_PIECES_ALL = 20
W = 2048
LANES = 128
SUBLANES = 8
MESH = pl.DeviceIdType.MESH


def constants():
    table = np.zeros((24, LANES), np.float32)
    theta = np.pi * (2.0 * np.arange(K) + 1.0) / (2.0 * K)
    degrees = np.arange(K)[:, None]
    scale = np.where(degrees == 0, 1.0, 2.0) / K
    table[:K, :K] = scale * np.cos(degrees * theta[None, :])
    table[K, :K] = np.cos(theta)
    numbers = np.arange(CODED_PIECES_ALL)
    table[K + 1, :CODED_PIECES_ALL] = np.cos(np.pi * (2.0 * numbers + 1.0) / (2.0 * CODED_PIECES_ALL))
    return table


def weights_into(table, alive, points_ref, w_ref):
    rows = lax.broadcasted_iota(jnp.int32, (K, LANES), 0)
    lanes = lax.broadcasted_iota(jnp.int32, (K, LANES), 1)
    number = jnp.zeros((K, LANES), jnp.int32)
    for i in range(K):
        number = jnp.where(rows == i, alive[i], number)
    nodes = jnp.broadcast_to(table[K + 1 : K + 2, :], (K, LANES))
    points = jnp.sum(jnp.where(lanes == number, nodes, 0.0), axis=1, keepdims=True)
    points = jnp.broadcast_to(points, (K, LANES))
    points_ref[...] = points
    samples = table[K : K + 1, :]
    over = jnp.ones((K, LANES), jnp.float32)
    under = jnp.ones((K, LANES), jnp.float32)
    for j in range(K):
        point = points_ref[j : j + 1, :]
        over = over * jnp.where(rows == j, 1.0, samples - point)
        under = under * jnp.where(rows == j, 1.0, points - point)
    lagrange = over / under
    for k in range(K):
        total = jnp.sum(lagrange * table[k : k + 1, :], axis=1, keepdims=True)
        w_ref[k] = jnp.broadcast_to(total, (K, LANES))


def each_in_half(me, count, half, act, unless=None):
    size = count // 2
    mine = me // size

    def run():
        @pl.when(mine != half)
        def _():
            act(half * size + lax.rem(me, size))

        for d in range(1, size):
            act(half * size + lax.rem(me + d, size))

    if unless is None:
        run()
    else:
        pl.when(unless == 0)(run)


def kernel(
    shares, rows,
    alive_hbm, starts_hbm, x_hbm, table_hbm, out,
    alive, starts, x, table, points, w, send_a, got_a, got_b, send_c,
    load_sems, a_send, a_recv, b_send, b_recv, c_send, c_recv, late_row, late_share,
):
    me_s = lax.axis_index("share")
    me_r = lax.axis_index("row")
    half_r, half_s = rows // 2, shares // 2
    late_r, late_s = me_r // half_r, me_s // half_s

    barrier = pltpu.get_barrier_semaphore()

    def greet_row(to):
        pl.semaphore_signal(barrier, inc=1, device_id=(me_s, to), device_id_type=MESH)

    def greet_share(to):
        pl.semaphore_signal(barrier, inc=1, device_id=(to, me_r), device_id_type=MESH)

    each_in_half(me_r, rows, 1, greet_row)
    each_in_half(me_s, shares, 1, greet_share)
    each_in_half(me_r, rows, 0, greet_row, unless=late_r)
    each_in_half(me_s, shares, 0, greet_share, unless=late_s)

    load_x = pltpu.make_async_copy(x_hbm, x, load_sems.at[0])
    load_starts = pltpu.make_async_copy(starts_hbm, starts, load_sems.at[1])
    load_alive = pltpu.make_async_copy(alive_hbm, alive, load_sems.at[2])
    load_table = pltpu.make_async_copy(table_hbm, table, load_sems.at[3])
    load_starts.start()
    load_x.start()
    load_alive.start()
    load_table.start()

    load_starts.wait()
    load_x.wait()
    for h in range(2):
        first = starts[h]
        for b in range(W // LANES):
            for t in range(x.shape[0]):
                send_a[h * (W // LANES) + b, t * SUBLANES : (t + 1) * SUBLANES] = x[t, first + b]

    pl.semaphore_wait(barrier, half_r - 1 + half_s - 1 + half_r * late_r + half_s * late_s)

    def announce_row(to):
        pl.semaphore_signal(late_row, inc=1, device_id=(me_s, to), device_id_type=MESH)

    def announce_share(to):
        pl.semaphore_signal(late_share, inc=1, device_id=(to, me_r), device_id_type=MESH)

    @pl.when(late_r == 1)
    def _():
        each_in_half(me_r, rows, 0, announce_row)

    @pl.when(late_s == 1)
    def _():
        each_in_half(me_s, shares, 0, announce_share)

    def spread_row(to):
        pltpu.make_async_remote_copy(
            src_ref=send_a.at[to], dst_ref=got_a.at[me_r],
            send_sem=a_send, recv_sem=a_recv.at[late_r], device_id=(me_s, to), device_id_type=MESH,
        ).start()

    each_in_half(me_r, rows, 0, spread_row)
    got_a[me_r] = send_a[me_r]

    @pl.when(late_r == 0)
    def _():
        pl.semaphore_wait(late_row, half_r)

    each_in_half(me_r, rows, 1, spread_row)

    load_alive.wait()
    load_table.wait()
    weights_into(table, alive, points, w)

    def waits(ref, send, recv):
        return pltpu.make_async_remote_copy(
            src_ref=ref, dst_ref=ref, send_sem=send, recv_sem=recv, device_id=(me_s, me_r), device_id_type=MESH
        )

    for c in range(2):

        @pl.when(late_r == c)
        def _():
            waits(got_a.at[pl.ds(0, half_r - 1)], a_send, a_recv.at[c]).wait_recv()

        @pl.when(late_r != c)
        def _():
            waits(got_a.at[pl.ds(0, half_r)], a_send, a_recv.at[c]).wait_recv()

        def spread_share(to):
            pltpu.make_async_remote_copy(
                src_ref=got_a.at[c * half_r + to], dst_ref=got_b.at[c, me_s],
                send_sem=b_send, recv_sem=b_recv.at[c], device_id=(to, me_r), device_id_type=MESH,
            ).start()

        each_in_half(me_s, shares, 0, spread_share)
        got_b[c, me_s] = got_a[c * half_r + me_s]
        if c == 0:

            @pl.when(late_s == 0)
            def _():
                pl.semaphore_wait(late_share, half_s)

        each_in_half(me_s, shares, 1, spread_share)

    for c in range(2):
        waits(got_b.at[c, pl.ds(0, shares - 1)], b_send, b_recv.at[c]).wait_recv()
        data = [got_b[c, i] for i in range(K)]
        for k in range(K):
            total = w[k, 0:1, :] * data[0]
            for i in range(1, K):
                total = total + w[k, i : i + 1, :] * data[i]
            send_c[c, k] = total

        def give_back(to):
            pltpu.make_async_remote_copy(
                src_ref=send_c.at[c, to], dst_ref=out.at[c * half_r + me_s],
                send_sem=c_send, recv_sem=c_recv, device_id=(to, me_r), device_id_type=MESH,
            ).start()

        each_in_half(me_s, shares, 0, give_back)
        each_in_half(me_s, shares, 1, give_back)
        out[c * half_r + me_s] = send_c[c, me_s]

    waits(got_a.at[pl.ds(0, rows - 1)], a_send, a_send).wait_send()
    waits(got_b.at[:, pl.ds(0, shares - 1)], b_send, b_send).wait_send()
    waits(send_c.at[:, pl.ds(0, shares - 1)], c_send, c_send).wait_send()
    waits(out.at[pl.ds(0, rows - 2)], c_send, c_recv).wait_recv()


def solution(mesh):
    shares, rows = mesh.shape["share"], mesh.shape["row"]
    table = constants()

    def body(remaining_coded_pieces, alive_piece_indices, slab_starting_positions):
        block, columns = remaining_coded_pieces.shape[1:]
        f32 = jnp.float32
        dma = pltpu.SemaphoreType.DMA
        tiled = remaining_coded_pieces.reshape(block // SUBLANES, SUBLANES, columns // LANES, LANES).transpose(0, 2, 1, 3)
        decoded = pl.pallas_call(
            functools.partial(kernel, shares, rows),
            out_shape=pltpu.VMEM((rows, block, LANES), f32),
            in_specs=[pl.BlockSpec(memory_space=pl.ANY)] * 4,
            out_specs=pl.BlockSpec(memory_space=pltpu.VMEM),
            scratch_shapes=[
                pltpu.SMEM((K,), jnp.int32),
                pltpu.SMEM((2,), jnp.int32),
                pltpu.VMEM((block // SUBLANES, columns // LANES, SUBLANES, LANES), f32),
                pltpu.VMEM((24, LANES), f32),
                pltpu.VMEM((K, LANES), f32),
                pltpu.VMEM((K, K, LANES), f32),
                pltpu.VMEM((rows, block, LANES), f32),
                pltpu.VMEM((rows, block, LANES), f32),
                pltpu.VMEM((2, shares, block, LANES), f32),
                pltpu.VMEM((2, shares, block, LANES), f32),
                dma((4,)),
                dma,
                dma((2,)),
                dma,
                dma((2,)),
                dma,
                dma,
                pltpu.SemaphoreType.REGULAR,
                pltpu.SemaphoreType.REGULAR,
            ],
            compiler_params=pltpu.CompilerParams(collective_id=0, has_side_effects=True),
            name="decode",
        )(alive_piece_indices, slab_starting_positions, tiled, jnp.asarray(table))
        return decoded.reshape(1, rows * block, LANES)

    return jax.shard_map(
        body, mesh=mesh, in_specs=(P("share", "row", None), P(), P()), out_specs=P("share", None, "row"), check_vma=False
    )
```

time: 45 us -> 40.9 us (0.909)
  the two profiles are of different devices: /device:TPU:1 before, /device:TPU:49 now
where the time goes in v2:
time: 40.9 us; the launch traced here: 40.8 us
  Pallas kernels  40.1 us (98%)
  local copies, waits for them, and re-layouts  0.71 us (2%)
    pallas_call x1, Pallas kernels, body(): pl.pallas_call(functools.partial(kernel, shares, rows), out_shape=pltpu.V...  40.1 us

profile of v2, /device:TPU:49, one launch (start us, length us, event | category | flops | bytes accessed | tf_op | source)
XLA Modules:
  0.0 40.8 jit_solution(10084104800831947937)
XLA Ops:
  0.0 40.1 %decode.1 = f32[32,16,128]{2,1,0:T(8,128)S(1)} custom-call(s32[16]{0:T(128)} %alive_hbm.1, s32[2]{0:T(128)} %starts_hbm.1, f32[2,64,8,128]{3,2,1,0:T(8,128)} %bitcast.5, f32[24,128]{1,0:T(8,128)} %constant.2.clone.table_hbm), custom_call_target="tpu_custom_call" | custom-call | tf_op jit(solution)/shard_map/decode/pallas_call | solution.py:213
  40.1 0.7 %copy.6 = f32[1,512,128]{2,1,0:T(8,128)} copy(f32[1,512,128]{2,1,0:T(8,128)S(1)} %bitcast.4) | data formatting | bytes 524288

commit v3 on v2

v3 whole, which is shorter than its diff:
```python
import jax
import jax.numpy as jnp
import numpy as np
from jax import lax
from jax.experimental import pallas as pl
from jax.experimental.pallas import tpu as pltpu
from jax.sharding import PartitionSpec as P

K = 16
CODED_PIECES_ALL = 20
W = 2048
LANES = 128
SUBLANES = 8
CHUNKS = 4
CHUNK_ORDER = (0, 1, 2, 3)
X, Y, Z, CORES = 4, 8, 8, 2
MESH = pl.DeviceIdType.MESH


def constants():
    table = np.zeros((24, LANES), np.float32)
    theta = np.pi * (2.0 * np.arange(K) + 1.0) / (2.0 * K)
    degrees = np.arange(K)[:, None]
    scale = np.where(degrees == 0, 1.0, 2.0) / K
    table[:K, :K] = scale * np.cos(degrees * theta[None, :])
    table[K, :K] = np.cos(theta)
    numbers = np.arange(CODED_PIECES_ALL)
    table[K + 1, :CODED_PIECES_ALL] = np.cos(np.pi * (2.0 * numbers + 1.0) / (2.0 * CODED_PIECES_ALL))
    return table


def weights_into(table, alive, points_ref, w_ref):
    rows = lax.broadcasted_iota(jnp.int32, (K, LANES), 0)
    lanes = lax.broadcasted_iota(jnp.int32, (K, LANES), 1)
    number = jnp.zeros((K, LANES), jnp.int32)
    for i in range(K):
        number = jnp.where(rows == i, alive[i], number)
    nodes = jnp.broadcast_to(table[K + 1 : K + 2, :], (K, LANES))
    points = jnp.sum(jnp.where(lanes == number, nodes, 0.0), axis=1, keepdims=True)
    points = jnp.broadcast_to(points, (K, LANES))
    points_ref[...] = points
    samples = table[K : K + 1, :]
    over = jnp.ones((K, LANES), jnp.float32)
    under = jnp.ones((K, LANES), jnp.float32)
    for j in range(K):
        point = points_ref[j : j + 1, :]
        over = over * jnp.where(rows == j, 1.0, samples - point)
        under = under * jnp.where(rows == j, 1.0, points - point)
    lagrange = over / under
    for k in range(K):
        total = jnp.sum(lagrange * table[k : k + 1, :], axis=1, keepdims=True)
        w_ref[k] = jnp.broadcast_to(total, (K, LANES))


def far_first(sizes):
    offsets = [(a, b) for a in range(sizes[0]) for b in range(sizes[1])]
    return sorted(offsets, key=lambda o: (-sum(min(d, n - d) for d, n in zip(o, sizes)), o))


SHARE_ORDER = far_first((Z, CORES))
HALF_Y = Y // 2


def each_in_half(me, size, half, act):
    @pl.when(me // size != half)
    def _():
        act(half * size + lax.rem(me, size))

    for d in range(1, size):
        act(half * size + lax.rem(me + d, size))


def kernel(
    alive_hbm, starts_hbm, x_hbm, table_hbm, out,
    alive, starts, x, table, points, w, send_a, got_a, got_b, send_c,
    load_sems, a_send, a_recv, b_send, b_recv, c_send, c_recv, below_sems, above_sems,
):
    shares, rows = Z * CORES, Y * X
    half_r, half_s = rows // 2, shares // 2
    sources = rows // CHUNKS
    step = got_b.shape[2]
    parts = got_a.shape[1] // step
    me_s = lax.axis_index("share")
    me_r = lax.axis_index("row")
    my_y, my_x = me_r // X, lax.rem(me_r, X)
    my_z, my_core = me_s // CORES, lax.rem(me_s, CORES)
    late = me_r // half_r
    place = lax.rem(my_y, HALF_Y)

    def share_at(dz, dc):
        return lax.rem(my_z + dz, Z) * CORES + lax.rem(my_core + dc, CORES)

    def tell(semaphore, share, row):
        pl.semaphore_signal(semaphore, inc=1, device_id=(share, row), device_id_type=MESH)

    barrier = pltpu.get_barrier_semaphore()

    load_x = pltpu.make_async_copy(x_hbm, x, load_sems.at[0])
    load_starts = pltpu.make_async_copy(starts_hbm, starts, load_sems.at[1])
    load_alive = pltpu.make_async_copy(alive_hbm, alive, load_sems.at[2])
    load_table = pltpu.make_async_copy(table_hbm, table, load_sems.at[3])
    load_starts.start()
    load_x.start()

    each_in_half(me_r, half_r, 0, lambda to: tell(barrier, me_s, to))

    @pl.when(late == 0)
    def _():
        each_in_half(me_r, half_r, 1, lambda to: tell(barrier, me_s, to))

    @pl.when(late == 1)
    def _():
        for dx in (2, 1, 3):
            tell(barrier, me_s, my_y * X + lax.rem(my_x + dx, X))

        @pl.when(place > 0)
        def _():
            tell(barrier, me_s, me_r - X)

        @pl.when(place < HALF_Y - 1)
        def _():
            tell(barrier, me_s, me_r + X)

    for offset in SHARE_ORDER[:-1]:
        tell(barrier, share_at(*offset), me_r)

    load_alive.start()
    load_table.start()
    load_starts.wait()
    load_x.wait()
    for h in range(2):
        first = starts[h]
        for b in range(W // LANES):
            for t in range(x.shape[0]):
                send_a[h * (W // LANES) + b, t * SUBLANES : (t + 1) * SUBLANES] = x[t, first + b]

    neighbours = 1 + lax.rem((place + 1) // 2, 2)
    pl.semaphore_wait(barrier, shares - 1 + (1 - late) * (rows - 1) + late * (half_r + X - 1 + neighbours))

    def spread_row(to):
        pltpu.make_async_remote_copy(
            src_ref=send_a.at[to], dst_ref=got_a.at[me_r],
            send_sem=a_send, recv_sem=a_recv.at[me_r // sources], device_id=(me_s, to), device_id_type=MESH,
        ).start()

    def spread_group(y):
        for dx in (2, 1, 3, 0):
            spread_row(y * X + lax.rem(my_x + dx, X))

    @pl.when(late == 0)
    def _():
        each_in_half(me_r, half_r, 0, spread_row)
        each_in_half(me_r, half_r, 1, spread_row)

    @pl.when(late == 1)
    def _():
        @pl.when(place > 0)
        def _():
            tell(above_sems.at[0], me_s, me_r - X)

        @pl.when(place < HALF_Y - 1)
        def _():
            tell(below_sems.at[0], me_s, me_r + X)

        each_in_half(me_r, half_r, 0, spread_row)
        for dx in (2, 1, 3):
            spread_row(my_y * X + lax.rem(my_x + dx, X))
        for j in range(1, HALF_Y):

            @pl.when(place >= j)
            def _():
                pl.semaphore_wait(below_sems.at[j - 1], 1)
                if j < HALF_Y - 1:

                    @pl.when(place < HALF_Y - 1)
                    def _():
                        tell(below_sems.at[j], me_s, me_r + X)

            @pl.when(place + j < HALF_Y)
            def _():
                pl.semaphore_wait(above_sems.at[j - 1], 1)
                if j < HALF_Y - 1:

                    @pl.when(place > 0)
                    def _():
                        tell(above_sems.at[j], me_s, me_r - X)

            @pl.when(place >= j)
            def _():
                spread_group(my_y - j)

            @pl.when(place + j < HALF_Y)
            def _():
                spread_group(my_y + j)

    got_a[me_r] = send_a[me_r]

    load_alive.wait()
    load_table.wait()
    weights_into(table, alive, points, w)

    def waits(ref, send, recv):
        return pltpu.make_async_remote_copy(
            src_ref=ref, dst_ref=ref, send_sem=send, recv_sem=recv, device_id=(me_s, me_r), device_id_type=MESH
        )

    def piece(c, owner):
        return c * sources + owner // parts, pl.ds(lax.rem(owner, parts) * step, step)

    for c in CHUNK_ORDER:

        @pl.when(me_r // sources == c)
        def _():
            waits(got_a.at[pl.ds(0, sources - 1)], a_send, a_recv.at[c]).wait_recv()

        @pl.when(me_r // sources != c)
        def _():
            waits(got_a.at[pl.ds(0, sources)], a_send, a_recv.at[c]).wait_recv()

        for offset in SHARE_ORDER[:-1]:
            to = share_at(*offset)
            pltpu.make_async_remote_copy(
                src_ref=got_a.at[*piece(c, to)], dst_ref=got_b.at[c, me_s],
                send_sem=b_send, recv_sem=b_recv.at[c], device_id=(to, me_r), device_id_type=MESH,
            ).start()
        got_b[c, me_s] = got_a[*piece(c, me_s)]

    for c in CHUNK_ORDER:
        waits(got_b.at[c, pl.ds(0, shares - 1)], b_send, b_recv.at[c]).wait_recv()
        for t in range(step // SUBLANES):
            part = slice(t * SUBLANES, (t + 1) * SUBLANES)
            data = [got_b[c, i, part] for i in range(K)]
            for k in range(K):
                total = w[k, 0:1, :] * data[0]
                for i in range(1, K):
                    total = total + w[k, i : i + 1, :] * data[i]
                send_c[c, k, part] = total

        def give_back(to):
            pltpu.make_async_remote_copy(
                src_ref=send_c.at[c, to], dst_ref=out.at[*piece(c, me_s)],
                send_sem=c_send, recv_sem=c_recv, device_id=(to, me_r), device_id_type=MESH,
            ).start()

        each_in_half(me_s, half_s, 0, give_back)
        each_in_half(me_s, half_s, 1, give_back)
        out[*piece(c, me_s)] = send_c[c, me_s]

    waits(got_a.at[pl.ds(0, rows - 1)], a_send, a_send).wait_send()
    waits(got_b.at[:, pl.ds(0, shares - 1)], b_send, b_send).wait_send()
    waits(send_c.at[:, pl.ds(0, shares - 1)], c_send, c_send).wait_send()
    waits(send_c.at[:, pl.ds(0, shares - 1)], c_send, c_recv).wait_recv()


def solution(mesh):
    shares, rows = mesh.shape["share"], mesh.shape["row"]
    table = constants()

    def body(remaining_coded_pieces, alive_piece_indices, slab_starting_positions):
        block, columns = remaining_coded_pieces.shape[1:]
        f32 = jnp.float32
        dma = pltpu.SemaphoreType.DMA
        tiled = remaining_coded_pieces.reshape(block // SUBLANES, SUBLANES, columns // LANES, LANES).transpose(0, 2, 1, 3)
        decoded = pl.pallas_call(
            kernel,
            out_shape=pltpu.VMEM((rows, block, LANES), f32),
            in_specs=[pl.BlockSpec(memory_space=pl.ANY)] * 4,
            out_specs=pl.BlockSpec(memory_space=pltpu.VMEM),
            scratch_shapes=[
                pltpu.SMEM((K,), jnp.int32),
                pltpu.SMEM((2,), jnp.int32),
                pltpu.VMEM((block // SUBLANES, columns // LANES, SUBLANES, LANES), f32),
                pltpu.VMEM((24, LANES), f32),
                pltpu.VMEM((K, LANES), f32),
                pltpu.VMEM((K, K, LANES), f32),
                pltpu.VMEM((rows, block, LANES), f32),
                pltpu.VMEM((rows, block, LANES), f32),
                pltpu.VMEM((CHUNKS, shares, 2 * block // CHUNKS, LANES), f32),
                pltpu.VMEM((CHUNKS, shares, 2 * block // CHUNKS, LANES), f32),
                dma((4,)),
                dma,
                dma((CHUNKS,)),
                dma,
                dma((CHUNKS,)),
                dma,
                dma,
                pltpu.SemaphoreType.REGULAR((HALF_Y - 1,)),
                pltpu.SemaphoreType.REGULAR((HALF_Y - 1,)),
            ],
            compiler_params=pltpu.CompilerParams(collective_id=0, has_side_effects=True),
            name="decode",
        )(alive_piece_indices, slab_starting_positions, tiled, jnp.asarray(table))
        return decoded.reshape(1, rows * block, LANES)

    return jax.shard_map(
        body, mesh=mesh, in_specs=(P("share", "row", None), P(), P()), out_specs=P("share", None, "row"), check_vma=False
    )
```

time: 40.9 us -> 36.3 us (0.89)
  the two profiles are of different devices: /device:TPU:49 before, /device:TPU:41 now
where the time goes in v3:
time: 36.3 us; the launch traced here: 36.2 us
  Pallas kernels  35.5 us (98%)
  local copies, waits for them, and re-layouts  0.71 us (2%)
    pallas_call x1, Pallas kernels, body(): pl.pallas_call(kernel, out_shape=pltpu.VMEM((rows, block, LANES), f32), i...  35.5 us

profile of v3, /device:TPU:41, one launch (start us, length us, event | category | flops | bytes accessed | tf_op | source)
XLA Modules:
  0.0 36.2 jit_solution(3781770183644380771)
XLA Ops:
  0.0 35.5 %decode.1 = f32[32,16,128]{2,1,0:T(8,128)S(1)} custom-call(s32[16]{0:T(128)} %alive_hbm.1, s32[2]{0:T(128)} %starts_hbm.1, f32[2,64,8,128]{3,2,1,0:T(8,128)} %bitcast.5, f32[24,128]{1,0:T(8,128)} %constant.2.clone.table_hbm), custom_call_target="tpu_custom_call" | custom-call | tf_op jit(solution)/shard_map/decode/pallas_call | solution.py:264
  35.5 0.7 %copy.6 = f32[1,512,128]{2,1,0:T(8,128)} copy(f32[1,512,128]{2,1,0:T(8,128)S(1)} %bitcast.4) | data formatting | bytes 524288

commit v4 on v3

--- a/solution.py
+++ b/solution.py
@@ -12,7 +12,6 @@
 LANES = 128
 SUBLANES = 8
 CHUNKS = 4
-CHUNK_ORDER = (0, 1, 2, 3)
 X, Y, Z, CORES = 4, 8, 8, 2
 MESH = pl.DeviceIdType.MESH
 
@@ -73,7 +72,7 @@
 def kernel(
     alive_hbm, starts_hbm, x_hbm, table_hbm, out,
     alive, starts, x, table, points, w, send_a, got_a, got_b, send_c,
-    load_sems, a_send, a_recv, b_send, b_recv, c_send, c_recv, below_sems, above_sems,
+    load_sems, a_send, a_recv, b_send, b_recv, c_send, c_recv, below_sems, above_sems, late_share,
 ):
     shares, rows = Z * CORES, Y * X
     half_r, half_s = rows // 2, shares // 2
@@ -102,11 +101,10 @@
     load_starts.start()
     load_x.start()
 
-    each_in_half(me_r, half_r, 0, lambda to: tell(barrier, me_s, to))
-
     @pl.when(late == 0)
     def _():
         each_in_half(me_r, half_r, 1, lambda to: tell(barrier, me_s, to))
+        each_in_half(me_r, half_r, 0, lambda to: tell(barrier, me_s, to))
 
     @pl.when(late == 1)
     def _():
@@ -121,8 +119,13 @@
         def _():
             tell(barrier, me_s, me_r + X)
 
-    for offset in SHARE_ORDER[:-1]:
-        tell(barrier, share_at(*offset), me_r)
+    late_s = me_s // half_s
+    each_in_half(me_s, half_s, 1, lambda to: tell(barrier, to, me_r))
+
+    @pl.when(late_s == 0)
+    def _():
+        each_in_half(me_s, half_s, 0, lambda to: tell(barrier, to, me_r))
+
 
     load_alive.start()
     load_table.start()
@@ -135,7 +138,11 @@
                 send_a[h * (W // LANES) + b, t * SUBLANES : (t + 1) * SUBLANES] = x[t, first + b]
 
     neighbours = 1 + lax.rem((place + 1) // 2, 2)
-    pl.semaphore_wait(barrier, shares - 1 + (1 - late) * (rows - 1) + late * (half_r + X - 1 + neighbours))
+    pl.semaphore_wait(barrier, half_s - 1 + half_s * late_s + half_r - 1 + late * (X + neighbours))
+
+    @pl.when(late_s == 1)
+    def _():
+        each_in_half(me_s, half_s, 0, lambda to: tell(late_share, to, me_r))
 
     def spread_row(to):
         pltpu.make_async_remote_copy(
@@ -150,18 +157,36 @@
     @pl.when(late == 0)
     def _():
         each_in_half(me_r, half_r, 0, spread_row)
-        each_in_half(me_r, half_r, 1, spread_row)
+
+        def from_below():
+            for j in range(2):
+                pl.semaphore_wait(below_sems.at[j], 1)
+
+                @pl.when(place < HALF_Y - 1)
+                def _():
+                    tell(below_sems.at[j], me_s, me_r + X)
+
+                spread_group(Y - 1 - j)
+
+        def from_above():
+            for j in range(2):
+                pl.semaphore_wait(above_sems.at[j], 1)
+
+                @pl.when(place > 0)
+                def _():
+                    tell(above_sems.at[j], me_s, me_r - X)
+
+                spread_group(HALF_Y + j)
+
+        pl.when(place < 2)(from_below)
+        from_above()
+        pl.when(place >= 2)(from_below)
 
     @pl.when(late == 1)
     def _():
-        @pl.when(place > 0)
-        def _():
-            tell(above_sems.at[0], me_s, me_r - X)
-
-        @pl.when(place < HALF_Y - 1)
-        def _():
-            tell(below_sems.at[0], me_s, me_r + X)
-
+        above, below = lax.rem(me_r + X, rows), me_r - X
+        tell(below_sems.at[0], me_s, above)
+        tell(above_sems.at[0], me_s, below)
         each_in_half(me_r, half_r, 0, spread_row)
         for dx in (2, 1, 3):
             spread_row(my_y * X + lax.rem(my_x + dx, X))
@@ -170,20 +195,24 @@
             @pl.when(place >= j)
             def _():
                 pl.semaphore_wait(below_sems.at[j - 1], 1)
-                if j < HALF_Y - 1:
+                if j == 1:
+                    tell(below_sems.at[1], me_s, above)
+                if j == 2:
 
                     @pl.when(place < HALF_Y - 1)
                     def _():
-                        tell(below_sems.at[j], me_s, me_r + X)
+                        tell(below_sems.at[2], me_s, above)
 
             @pl.when(place + j < HALF_Y)
             def _():
                 pl.semaphore_wait(above_sems.at[j - 1], 1)
-                if j < HALF_Y - 1:
+                if j == 1:
+                    tell(above_sems.at[1], me_s, below)
+                if j == 2:
 
                     @pl.when(place > 0)
                     def _():
-                        tell(above_sems.at[j], me_s, me_r - X)
+                        tell(above_sems.at[2], me_s, below)
 
             @pl.when(place >= j)
             def _():
@@ -207,7 +236,8 @@
     def piece(c, owner):
         return c * sources + owner // parts, pl.ds(lax.rem(owner, parts) * step, step)
 
-    for c in CHUNK_ORDER:
+    for n in range(CHUNKS):
+        c = lax.rem(n + CHUNKS // 2 * late, CHUNKS)
 
         @pl.when(me_r // sources == c)
         def _():
@@ -217,15 +247,24 @@
         def _():
             waits(got_a.at[pl.ds(0, sources)], a_send, a_recv.at[c]).wait_recv()
 
-        for offset in SHARE_ORDER[:-1]:
-            to = share_at(*offset)
+        def spread_share(to):
             pltpu.make_async_remote_copy(
                 src_ref=got_a.at[*piece(c, to)], dst_ref=got_b.at[c, me_s],
                 send_sem=b_send, recv_sem=b_recv.at[c], device_id=(to, me_r), device_id_type=MESH,
             ).start()
+
+        each_in_half(me_s, half_s, 0, spread_share)
+        if n == 0:
+
+            @pl.when(late_s == 0)
+            def _():
+                pl.semaphore_wait(late_share, half_s)
+
+        each_in_half(me_s, half_s, 1, spread_share)
         got_b[c, me_s] = got_a[*piece(c, me_s)]
 
-    for c in CHUNK_ORDER:
+    for n in range(CHUNKS):
+        c = lax.rem(n + CHUNKS // 2 * late, CHUNKS)
         waits(got_b.at[c, pl.ds(0, shares - 1)], b_send, b_recv.at[c]).wait_recv()
         for t in range(step // SUBLANES):
             part = slice(t * SUBLANES, (t + 1) * SUBLANES)
@@ -286,6 +325,7 @@
                 dma,
                 pltpu.SemaphoreType.REGULAR((HALF_Y - 1,)),
                 pltpu.SemaphoreType.REGULAR((HALF_Y - 1,)),
+                pltpu.SemaphoreType.REGULAR,
             ],
             compiler_params=pltpu.CompilerParams(collective_id=0, has_side_effects=True),
             name="decode",

time: 36.3 us -> 35.2 us (0.970)
  the two profiles are of different devices: /device:TPU:41 before, /device:TPU:1 now
where the time goes in v4:
time: 35.2 us; the launch traced here: 35 us
  Pallas kernels  34.3 us (97%)
  local copies, waits for them, and re-layouts  0.71 us (2%)
    pallas_call x1, Pallas kernels, body(): pl.pallas_call(kernel, out_shape=pltpu.VMEM((rows, block, LANES), f32), i...  34.3 us
    unnamed x1, local copies, waits for them, and re-layouts  0.71 us

profile of v4, /device:TPU:1, one launch (start us, length us, event | category | flops | bytes accessed | tf_op | source)
XLA Modules:
  0.0 35.0 jit_solution(10031285331747460020)
XLA Ops:
  0.0 34.3 %decode.1 = f32[32,16,128]{2,1,0:T(8,128)S(1)} custom-call(s32[16]{0:T(128)} %alive_hbm.1, s32[2]{0:T(128)} %starts_hbm.1, f32[2,64,8,128]{3,2,1,0:T(8,128)} %bitcast.5, f32[24,128]{1,0:T(8,128)} %constant.2.clone.table_hbm), custom_call_target="tpu_custom_call" | custom-call | tf_op jit(solution)/shard_map/decode/pallas_call | solution.py:303
  34.3 0.7 %copy.6 = f32[1,512,128]{2,1,0:T(8,128)} copy(f32[1,512,128]{2,1,0:T(8,128)S(1)} %bitcast.4) | data formatting | bytes 524288

commit v5 on v4

--- a/solution.py
+++ b/solution.py
@@ -58,6 +58,8 @@
 
 SHARE_ORDER = far_first((Z, CORES))
 HALF_Y = Y // 2
+LOW = (3, 2, 0, 1)
+HIGH = (0, 1, 2, 3)
 
 
 def each_in_half(me, size, half, act):
@@ -72,7 +74,7 @@
 def kernel(
     alive_hbm, starts_hbm, x_hbm, table_hbm, out,
     alive, starts, x, table, points, w, send_a, got_a, got_b, send_c,
-    load_sems, a_send, a_recv, b_send, b_recv, c_send, c_recv, below_sems, above_sems, late_share,
+    load_sems, a_send, a_recv, b_send, b_recv, c_send, c_recv, below_sems, above_sems, late_share, group_sems,
 ):
     shares, rows = Z * CORES, Y * X
     half_r, half_s = rows // 2, shares // 2
@@ -158,35 +160,25 @@
     def _():
         each_in_half(me_r, half_r, 0, spread_row)
 
-        def from_below():
-            for j in range(2):
-                pl.semaphore_wait(below_sems.at[j], 1)
-
-                @pl.when(place < HALF_Y - 1)
-                def _():
-                    tell(below_sems.at[j], me_s, me_r + X)
-
-                spread_group(Y - 1 - j)
-
-        def from_above():
-            for j in range(2):
-                pl.semaphore_wait(above_sems.at[j], 1)
-
-                @pl.when(place > 0)
-                def _():
-                    tell(above_sems.at[j], me_s, me_r - X)
-
-                spread_group(HALF_Y + j)
-
-        pl.when(place < 2)(from_below)
-        from_above()
-        pl.when(place >= 2)(from_below)
+        for n in range(HALF_Y):
+            group = jnp.where(place < 2, LOW[n], HIGH[n])
+            pl.semaphore_wait(group_sems.at[group], 1)
+            spread_group(HALF_Y + group)
 
     @pl.when(late == 1)
     def _():
         above, below = lax.rem(me_r + X, rows), me_r - X
-        tell(below_sems.at[0], me_s, above)
-        tell(above_sems.at[0], me_s, below)
+        for early in range(HALF_Y):
+            tell(group_sems.at[place], me_s, early * X + my_x)
+
+        @pl.when(place < HALF_Y - 1)
+        def _():
+            tell(below_sems.at[0], me_s, above)
+
+        @pl.when(place > 0)
+        def _():
+            tell(above_sems.at[0], me_s, below)
+
         each_in_half(me_r, half_r, 0, spread_row)
         for dx in (2, 1, 3):
             spread_row(my_y * X + lax.rem(my_x + dx, X))
@@ -195,24 +187,20 @@
             @pl.when(place >= j)
             def _():
                 pl.semaphore_wait(below_sems.at[j - 1], 1)
-                if j == 1:
-                    tell(below_sems.at[1], me_s, above)
-                if j == 2:
+                if j < HALF_Y - 1:
 
                     @pl.when(place < HALF_Y - 1)
                     def _():
-                        tell(below_sems.at[2], me_s, above)
+                        tell(below_sems.at[j], me_s, above)
 
             @pl.when(place + j < HALF_Y)
             def _():
                 pl.semaphore_wait(above_sems.at[j - 1], 1)
-                if j == 1:
-                    tell(above_sems.at[1], me_s, below)
-                if j == 2:
+                if j < HALF_Y - 1:
 
                     @pl.when(place > 0)
                     def _():
-                        tell(above_sems.at[2], me_s, below)
+                        tell(above_sems.at[j], me_s, below)
 
             @pl.when(place >= j)
             def _():
@@ -236,8 +224,15 @@
     def piece(c, owner):
         return c * sources + owner // parts, pl.ds(lax.rem(owner, parts) * step, step)
 
+    pair = me_r // sources
+    across = CHUNKS - 1 - pair
+
+    def chunk_at(n):
+        near = pair if n < 2 else across
+        return near if n % 2 == 0 else near + 1 - 2 * lax.rem(near, 2)
+
     for n in range(CHUNKS):
-        c = lax.rem(n + CHUNKS // 2 * late, CHUNKS)
+        c = chunk_at(n)
 
         @pl.when(me_r // sources == c)
         def _():
@@ -264,7 +259,7 @@
         got_b[c, me_s] = got_a[*piece(c, me_s)]
 
     for n in range(CHUNKS):
-        c = lax.rem(n + CHUNKS // 2 * late, CHUNKS)
+        c = chunk_at(n)
         waits(got_b.at[c, pl.ds(0, shares - 1)], b_send, b_recv.at[c]).wait_recv()
         for t in range(step // SUBLANES):
             part = slice(t * SUBLANES, (t + 1) * SUBLANES)
@@ -326,6 +321,7 @@
                 pltpu.SemaphoreType.REGULAR((HALF_Y - 1,)),
                 pltpu.SemaphoreType.REGULAR((HALF_Y - 1,)),
                 pltpu.SemaphoreType.REGULAR,
+                pltpu.SemaphoreType.REGULAR((HALF_Y,)),
             ],
             compiler_params=pltpu.CompilerParams(collective_id=0, has_side_effects=True),
             name="decode",

time: 35.2 us -> 34.3 us (0.974)
  Pallas kernels: 34.3 us -> 33.5 us
    pallas_call x1, Pallas kernels: 34.3 us -> 33.5 us  [body(): pl.pallas_call(kernel, out_shape=pltpu.VMEM((rows, block, LANES), f32), i...]
where the time goes in v5:
time: 34.3 us; the launch traced here: 34.2 us
  Pallas kernels  33.5 us (98%)
  local copies, waits for them, and re-layouts  0.71 us (2%)
    pallas_call x1, Pallas kernels, body(): pl.pallas_call(kernel, out_shape=pltpu.VMEM((rows, block, LANES), f32), i...  33.5 us
    unnamed x1, local copies, waits for them, and re-layouts  0.71 us

profile of v5, /device:TPU:1, one launch (start us, length us, event | category | flops | bytes accessed | tf_op | source)
XLA Modules:
  0.0 34.2 jit_solution(12580711381986247448)
XLA Ops:
  0.0 33.5 %decode.1 = f32[32,16,128]{2,1,0:T(8,128)S(1)} custom-call(s32[16]{0:T(128)} %alive_hbm.1, s32[2]{0:T(128)} %starts_hbm.1, f32[2,64,8,128]{3,2,1,0:T(8,128)} %bitcast.5, f32[24,128]{1,0:T(8,128)} %constant.2.clone.table_hbm), custom_call_target="tpu_custom_call" | custom-call | tf_op jit(solution)/shard_map/decode/pallas_call | solution.py:298
  33.5 0.7 %copy.6 = f32[1,512,128]{2,1,0:T(8,128)} copy(f32[1,512,128]{2,1,0:T(8,128)S(1)} %bitcast.4) | data formatting | bytes 524288

commit v6 on v5

--- a/solution.py
+++ b/solution.py
@@ -179,7 +179,9 @@
         def _():
             tell(above_sems.at[0], me_s, below)
 
-        each_in_half(me_r, half_r, 0, spread_row)
+        for y in (0, 1, 2, 3):
+            spread_group(y)
+
         for dx in (2, 1, 3):
             spread_row(my_y * X + lax.rem(my_x + dx, X))
         for j in range(1, HALF_Y):

time: 34.3 us -> 34.4 us (level); the launches traced: 34.2 us -> 33.9 us
  no operation moved by 1% of the time
where the time goes in v6:
time: 34.4 us; the launch traced here: 33.9 us
  Pallas kernels  33.2 us (97%)
  local copies, waits for them, and re-layouts  0.71 us (2%)
    pallas_call x1, Pallas kernels, body(): pl.pallas_call(kernel, out_shape=pltpu.VMEM((rows, block, LANES), f32), i...  33.2 us
    unnamed x1, local copies, waits for them, and re-layouts  0.71 us

profile of v6, /device:TPU:1, one launch (start us, length us, event | category | flops | bytes accessed | tf_op | source)
XLA Modules:
  0.0 33.9 jit_solution(8833278660536456501)
XLA Ops:
  0.0 33.2 %decode.1 = f32[32,16,128]{2,1,0:T(8,128)S(1)} custom-call(s32[16]{0:T(128)} %alive_hbm.1, s32[2]{0:T(128)} %starts_hbm.1, f32[2,64,8,128]{3,2,1,0:T(8,128)} %bitcast.5, f32[24,128]{1,0:T(8,128)} %constant.2.clone.table_hbm), custom_call_target="tpu_custom_call" | custom-call | tf_op jit(solution)/shard_map/decode/pallas_call | solution.py:300
  33.2 0.7 %copy.6 = f32[1,512,128]{2,1,0:T(8,128)} copy(f32[1,512,128]{2,1,0:T(8,128)S(1)} %bitcast.4) | data formatting | bytes 524288

commit v7 on v6

--- a/solution.py
+++ b/solution.py
@@ -153,8 +153,8 @@
         ).start()
 
     def spread_group(y):
-        for dx in (2, 1, 3, 0):
-            spread_row(y * X + lax.rem(my_x + dx, X))
+        for column in range(X):
+            spread_row(y * X + column)
 
     @pl.when(late == 0)
     def _():

time: 34.4 us -> 34.4 us (level)
  no operation moved by 1% of the time
where the time goes in v7:
time: 34.4 us; the launch traced here: 34.2 us
  Pallas kernels  33.5 us (97%)
  local copies, waits for them, and re-layouts  0.71 us (2%)
    pallas_call x1, Pallas kernels, body(): pl.pallas_call(kernel, out_shape=pltpu.VMEM((rows, block, LANES), f32), i...  33.5 us
    unnamed x1, local copies, waits for them, and re-layouts  0.71 us

profile of v7, /device:TPU:1, one launch (start us, length us, event | category | flops | bytes accessed | tf_op | source)
XLA Modules:
  0.0 34.2 jit_solution(10794895108633426108)
XLA Ops:
  0.0 33.5 %decode.1 = f32[32,16,128]{2,1,0:T(8,128)S(1)} custom-call(s32[16]{0:T(128)} %alive_hbm.1, s32[2]{0:T(128)} %starts_hbm.1, f32[2,64,8,128]{3,2,1,0:T(8,128)} %bitcast.5, f32[24,128]{1,0:T(8,128)} %constant.2.clone.table_hbm), custom_call_target="tpu_custom_call" | custom-call | tf_op jit(solution)/shard_map/decode/pallas_call | solution.py:300
  33.5 0.7 %copy.6 = f32[1,512,128]{2,1,0:T(8,128)} copy(f32[1,512,128]{2,1,0:T(8,128)S(1)} %bitcast.4) | data formatting | bytes 524288
